TPU v7x, 256 devices: a whole 4x4x8 slice. The times are simulated.
256 devices in a mesh: dp: 32 (over x_hi, z, core), tensor: 8 (over y, x_lo).
Axes of the slice: x: 4 (x_hi: 2, x_lo: 2; x = x_hi * 2 + x_lo), y: 4, z: 8, core: 2. Of those that a mesh axis runs over, the one named last changes fastest.
Arguments:
- grad_hidden: bfloat16 [4096, 14336], P('dp', 'tensor'), may hold values from -18 to 18
- gate: bfloat16 [4096, 14336], P('dp', 'tensor'), may hold values from -6 to 6
Outputs:
- factor: float32 [14336, 14336], P('tensor', 'dp')
All inputs are finite; a program needn't handle non-finite values.
Results may differ from a plain program's by a relative error of at most 0.0065.
Values may be sent and summed in bfloat16 or wider, within the bound.
A program may use at most 128 MiB of HBM per device.

v0:
```python
import jax
import jax.numpy as jnp
from jax import lax
from jax.sharding import PartitionSpec as P

FF = 14336


def broadcast(block, axis, owner):
    block = jnp.where(lax.axis_index(axis) == owner, block, jnp.zeros_like(block))
    return lax.psum(block, axis)


def shards(grad_hidden, gate):
    up_grad = (grad_hidden.astype(jnp.float32) * jax.nn.silu(gate.astype(jnp.float32))).astype(
        jnp.bfloat16
    )
    tensor_count = lax.axis_size("tensor")
    data_count = lax.axis_size("dp")
    col_width = FF // data_count
    ratio = data_count // tensor_count
    data_index = lax.axis_index("dp")
    owner = data_index // ratio
    offset = data_index % ratio * col_width
    contract = (((0,), (0,)), ((), ()))
    total_tokens = up_grad.shape[0] * data_count
    rows_all = lax.all_gather(up_grad, "dp", axis=0, tiled=True)
    panel = lax.dynamic_slice_in_dim(rows_all, offset, col_width, 1)
    cols_all = broadcast(panel, "tensor", owner)
    summed = lax.dot_general(rows_all, cols_all, contract, preferred_element_type=jnp.float32)
    return summed / total_tokens


def solution(mesh):
    return jax.shard_map(
        shards,
        mesh=mesh,
        in_specs=(P("dp", "tensor"), P("dp", "tensor")),
        out_specs=P("tensor", "dp"),
        check_vma=False,
    )
```

profile of v0, /device:TPU:1, one launch (start us, length us, event | category | flops | bytes accessed | tf_op | source)
XLA Modules:
  0.0 352.8 jit_solution(12489471338623991828)
XLA Ops:
  6.5 0.0 all-gather.2.cloned.1.call-start
  6.5 2.2 fusion.4
  8.7 0.0 all-gather.2.cloned.1.call-update
  8.8 0.0 all-reduce.2.cloned.1.call-start
  8.8 132.4 %all-gather.2.cloned.1.call-done = bf16[4096,1792]{1,0:T(8,128)(2,1)} async-done(((bf16[128,1792]{1,0:T(8,128)(2,1)}), bf16[4096,1792]{1,0:T(8,128)(2,1)}) %all-gather.2.cloned.1.call-update) | async-done | bytes 14680080 | tf_op jit(solution)/shard_map/all_gather | solution.py:27
  141.3 7.3 %dynamic-slice_select_fusion = bf16[4096,448]{1,0:T(8,128)(2,1)} fusion(bf16[4096,1792]{1,0:T(8,128)(2,1)} %all-gather.2.cloned.1.call-done, s32[]{:T(128)S(6)} %select_n.25, pred[]{:T(512)S(6)} %eq.5), kind=kLoop, calls=%fused_computation | loop fusion | flops 1835008 | bytes 7340037 | tf_op jit(solution)/shard_map/jit(_where)/select_n | solution.py:10
  148.6 0.0 all-reduce.2.cloned.1.call-update
  148.6 184.0 %all-reduce.2.cloned.1.call-done = bf16[4096,448]{1,0:T(8,128)(2,1)} async-done(((bf16[4096,448]{1,0:T(8,128)(2,1)}), bf16[4096,448]{1,0:T(8,128)(2,1)}) %all-reduce.2.cloned.1.call-update) | async-done | bytes 3670032 | tf_op jit(solution)/shard_map/psum | solution.py:11
  332.6 13.4 %convolution_multiply_fusion = f32[1792,448]{0,1:T(8,128)} fusion(bf16[4096,1792]{1,0:T(8,128)(2,1)} %all-gather.2.cloned.1.call-done, bf16[4096,448]{1,0:T(8,128)(2,1)} %all-reduce.2.cloned.1.call-done), kind=kOutput, calls=%fused_computation.1 | convolution fusion | flops 6577471488 | bytes 21561344 | tf_op jit(solution)/shard_map/dot_general | solution.py:30
Async XLA Ops:
  6.5 134.7 %all-gather.2.cloned.1.call-start = ((), (), s32[]{:S(2)}) async-start(), calls=%async_computation | async-start | bytes 15138816 | tf_op jit(solution)/shard_map/all_gather | solution.py:27
  8.8 323.8 %all-reduce.2.cloned.1.call-start = ((), (), s32[]{:S(2)}) async-start(), calls=%async_computation.1 | async-start | bytes 8388608 | tf_op jit(solution)/shard_map/psum | solution.py:11
Sparse Core Ops, SparseCore 0:
  10.1 131.1 all-gather.1
  148.7 183.7 all-reduce.1
where the time goes:
time: 353 us
  waiting for transfers between devices  316 us (90%)
  matrix products  13.4 us (4%)
  between operations  13.4 us (4%)
  other arithmetic  9.53 us (3%)
    psum x1, waiting for transfers between devices, broadcast(): return lax.psum(block, axis)  184 us
    all_gather x1, waiting for transfers between devices, shards(): rows_all = lax.all_gather(up_grad, 'dp', axis=0, tiled=True)  132 us
    dot_general x1, matrix products, shards(): lax.dot_general(rows_all, cols_all, contract, preferred_element_type=jnp....  13.4 us
    select_n x1, other arithmetic, broadcast(): jnp.where(lax.axis_index(axis) == owner, block, jnp.zeros_like(block))  7.33 us
  transfers between devices with their start and end apart: 2, of which 2 were waited for; matrix products, arithmetic and copies ran while one was open for 0% of the time, Pallas kernels for 0%

commit v1 on v0

v1 whole, which is shorter than its diff:
```python
import jax
import jax.numpy as jnp
from jax import lax
from jax.experimental import pallas as pl
from jax.experimental.pallas import tpu as pltpu
from jax.sharding import PartitionSpec as P

WIDTH = 1792
TOK = 128
UNITS = 16
PIECE = 112
COLS = 448
CUT = 896
A, B = 0, 1
SPAN = (pl.ds(0, CUT), pl.ds(CUT, WIDTH - CUT))
TILE = 256
NT = (((1,), (1,)), ((), ()))


def kernel(
    grad_ref, gate_ref, out_ref, rows, rows_o, cols, cols_o,
    row_recv, rowo_recv, spread_recv, piece_recv, colo_recv, ssem,
):
    dp, tn = lax.axis_index("dp"), lax.axis_index("tensor")
    core, z, xh = lax.rem(dp, 2), lax.rem(lax.div(dp, 2), 8), lax.div(dp, 16)
    y, xl = lax.div(tn, 2), lax.rem(tn, 2)

    def device(h, k, c, t):
        return (h * 16 + k * 2 + c, t)

    def ring(value, size):
        return lax.rem(value + size, size)

    z_up = device(xh, ring(z + 1, 8), core, tn)
    z_dn = device(xh, ring(z - 1, 8), core, tn)
    x_far = device(1 - xh, z, core, tn)
    x_near = device(xh, z, core, y * 2 + 1 - xl)
    y_up = device(xh, z, core, ring(y + 1, 4) * 2 + xl)
    y_dn = device(xh, z, core, ring(y - 1, 4) * 2 + xl)
    other = device(xh, z, 1 - core, tn)

    def unit(h, k):
        return h * 8 + ring(k, 8)

    me = unit(xh, z)
    block = xh * 4 + lax.div(z, 2)
    inside = (block == tn).astype(jnp.int32)

    barrier = pltpu.get_barrier_semaphore()

    def greet(target):
        pl.semaphore_signal(barrier, inc=1, device_id=target, device_id_type=pl.DeviceIdType.MESH)

    for target in (z_up, z_dn, x_far, x_near, y_up, y_dn, other):
        greet(target)
    for h in range(2):
        for k in range(8):
            @pl.when(jnp.logical_or(inside == 0, me != h * 8 + k))
            def _():
                greet(device(h, k, core, block))

    up_grad = (
        grad_ref[...].astype(jnp.float32) * jax.nn.silu(gate_ref[...].astype(jnp.float32))
    ).astype(jnp.bfloat16)
    rows[me] = up_grad.T

    pl.semaphore_wait(barrier, 23 - inside)

    sent = []

    def copy(src, dst, recv, target):
        made = pltpu.make_async_remote_copy(
            src_ref=src, dst_ref=dst, send_sem=ssem.at[len(sent)], recv_sem=recv,
            device_id=target, device_id_type=pl.DeviceIdType.MESH,
        )
        sent.append(None)
        return made

    waits = []

    def send(src, dst, recv, target):
        made = copy(src, dst, recv, target)
        made.start()
        waits.append(made.wait_send)

    def send_when(cond, src, dst, recv, target):
        made = copy(src, dst, recv, target)
        pl.when(cond)(made.start)
        waits.append(lambda: pl.when(cond)(made.wait_send))

    def arrive(ref, recv):
        pltpu.make_async_remote_copy(
            src_ref=ref, dst_ref=ref, send_sem=ssem.at[0], recv_sem=recv,
            device_id=other, device_id_type=pl.DeviceIdType.MESH,
        ).wait_recv()

    half_x, half_p = lax.div(tn, 4), lax.rem(tn, 4)
    for m in range(2):
        target_z = half_p * 2 + m
        for e in range(8):
            src = rows.at[me, pl.ds(m * 896 + e * PIECE, PIECE)]
            mine = jnp.logical_and(me == unit(half_x, target_z), tn == e)
            send_when(
                jnp.logical_not(mine), src, cols.at[e, me], spread_recv.at[me],
                device(half_x, target_z, core, e),
            )

            @pl.when(mine)
            def _():
                cols[e, me] = rows[me, pl.ds(m * 896 + e * PIECE, PIECE), :]

    def row(kind, u, *targets):
        ref = rows.at[u, SPAN[kind]]
        for target in targets:
            send(ref, ref, row_recv.at[kind, u], target)
        send(ref, rows_o.at[u, SPAN[kind]], rowo_recv.at[kind, u], other)

    def row_in(kind, u, *targets):
        arrive(rows.at[u, SPAN[kind]], row_recv.at[kind, u])
        row(kind, u, *targets)

    def piece(e, *targets):
        for target in targets:
            send(cols.at[e], cols.at[e], piece_recv.at[e], target)
        slot = lax.rem(e, 4)
        send_when(lax.div(e, 4) != core, cols.at[e], cols_o.at[slot], colo_recv.at[slot], other)

    def piece_in(e, *targets):
        arrive(cols.at[e], piece_recv.at[e])
        piece(e, *targets)

    row(B, me, x_far, z_up, z_dn)
    row(A, me, x_far, z_up, z_dn)

    for u in range(UNITS):
        @pl.when(jnp.logical_or(inside == 0, me != u))
        def _():
            arrive(cols.at[tn, u], spread_recv.at[u])
    piece(tn, x_near, y_up, y_dn)

    far = unit(1 - xh, z)
    row_in(B, far, z_up, z_dn)
    row_in(A, far)

    near_piece = y * 2 + 1 - xl
    dn, up, opp = ring(y - 1, 4) * 2, ring(y + 1, 4) * 2, ring(y + 2, 4) * 2
    for j in range(1, 4):
        lo, hi = unit(xh, z - j), unit(xh, z + j)
        far_lo, far_hi = unit(1 - xh, z - j), unit(1 - xh, z + j)
        row_in(B, lo, *((z_up,) if j < 3 else ()))
        row_in(B, hi, z_dn)
        row_in(A, lo, x_far, z_up)
        row_in(A, hi, x_far, *((z_dn,) if j < 3 else ()))
        if j == 1:
            piece_in(near_piece, y_up, y_dn)
        if j == 2:
            piece_in(dn + xl, y_up)
            piece_in(up + xl)
        if j == 3:
            piece_in(dn + 1 - xl)
            piece_in(up + 1 - xl, y_dn)
        row_in(B, far_lo, z_up)
        row_in(B, far_hi, *((z_dn,) if j < 3 else ()))
        if j > 1:
            row_in(A, unit(1 - xh, z - j + 1))
            row_in(A, unit(1 - xh, z + j - 1))

    piece_in(opp + xl)
    piece_in(opp + 1 - xl)

    def ready(units):
        for u in units:
            for kind in (A, B):
                arrive(rows_o.at[u, SPAN[kind]], rowo_recv.at[kind, u])

    def multiply(units, first=False, last=False):
        ready(units)
        right = jnp.concatenate(
            [
                panel.reshape(COLS, TOK)
                for u in units
                for panel in (cols[pl.ds(core * 4, 4), u], cols_o[:, u])
            ],
            axis=1,
        )

        def tile(i, _):
            span = pl.ds(pl.multiple_of(i * TILE, TILE), TILE)
            left = jnp.concatenate([r[u, span, :] for u in units for r in (rows, rows_o)], axis=1)
            total = lax.dot_general(left, right, NT, preferred_element_type=jnp.float32)
            if not first:
                total = total + out_ref[span, :]
            if last:
                total = total * (1.0 / 4096)
            out_ref[span, :] = total
            return 0

        lax.fori_loop(0, WIDTH // TILE, tile, 0)

    for slot in range(4):
        arrive(cols_o.at[slot], colo_recv.at[slot])

    def around(j):
        return [unit(h, k) for h in (xh, 1 - xh) for k in (z - j, z + j)]

    multiply([me, far], first=True)
    multiply(around(1))
    multiply(around(2))
    last, far_last = unit(xh, z + 4), unit(1 - xh, z + 4)
    row_in(A, last, x_far)
    row_in(B, last)
    row_in(B, far_last)
    row_in(A, unit(1 - xh, z - 3))
    row_in(A, unit(1 - xh, z + 3))
    multiply(around(3))
    row_in(A, far_last)
    multiply([last, far_last], last=True)

    for wait in waits:
        wait()


def shards(grad_hidden, gate):
    vmem = pl.BlockSpec(memory_space=pltpu.VMEM)
    return pl.pallas_call(
        kernel,
        out_shape=jax.ShapeDtypeStruct((WIDTH, COLS), jnp.float32),
        in_specs=[vmem] * 2,
        out_specs=vmem,
        scratch_shapes=[
            pltpu.VMEM((UNITS, WIDTH, TOK), jnp.bfloat16),
            pltpu.VMEM((UNITS, WIDTH, TOK), jnp.bfloat16),
            pltpu.VMEM((8, UNITS, PIECE, TOK), jnp.bfloat16),
            pltpu.VMEM((4, UNITS, PIECE, TOK), jnp.bfloat16),
            pltpu.SemaphoreType.DMA((2, UNITS)),
            pltpu.SemaphoreType.DMA((2, UNITS)),
            pltpu.SemaphoreType.DMA((UNITS,)),
            pltpu.SemaphoreType.DMA((8,)),
            pltpu.SemaphoreType.DMA((4,)),
            pltpu.SemaphoreType.DMA((128,)),
        ],
        compiler_params=pltpu.CompilerParams(
            collective_id=0, has_side_effects=True, vmem_limit_bytes=56 * 1024 * 1024
        ),
    )(grad_hidden, gate)


def solution(mesh):
    return jax.shard_map(
        shards,
        mesh=mesh,
        in_specs=(P("dp", "tensor"), P("dp", "tensor")),
        out_specs=P("tensor", "dp"),
        check_vma=False,
    )
```

time: 353 us -> 121 us (0.34)
  the two profiles are of different devices: /device:TPU:1 before, /device:TPU:9 now
where the time goes in v1:
time: 121 us
  Pallas kernels  116 us (96%)
  local copies, waits for them, and re-layouts  5.04 us (4%)
    pallas_call x1, Pallas kernels, shards(): pl.pallas_call(kernel, out_shape=jax.ShapeDtypeStruct((WIDTH, COLS), jnp....  116 us
    pallas_call x1, local copies, waits for them, and re-layouts, shards(): pl.pallas_call(kernel, out_shape=jax.ShapeDtypeStruct((WIDTH, COLS), jnp....  5.04 us

profile of v1, /device:TPU:9, one launch (start us, length us, event | category | flops | bytes accessed | tf_op | source)
XLA Modules:
  0.0 120.8 jit_solution(2670997172223876612)
XLA Ops:
  0.0 115.7 %shard_map.28 = f32[1792,448]{1,0:T(8,128)} custom-call(bf16[128,1792]{1,0:T(8,128)(2,1)} %grad_ref.1, bf16[128,1792]{1,0:T(8,128)(2,1)} %gate_ref.1), custom_call_target="tpu_custom_call" | custom-call | tf_op jit(solution)/shard_map/pallas_call | solution.py:225
  115.7 5.0 %copy.3 = f32[1792,448]{0,1:T(8,128)} copy(f32[1792,448]{1,0:T(8,128)} %shard_map.28) | data formatting | bytes 6422528 | tf_op jit(solution)/shard_map/pallas_call | solution.py:225

commit v2 on v1

v2 whole, which is shorter than its diff:
```python
import jax
import jax.numpy as jnp
from jax import lax
from jax.experimental import pallas as pl
from jax.experimental.pallas import tpu as pltpu
from jax.sharding import PartitionSpec as P

WIDTH = 1792
TOK = 128
UNITS = 16
PIECE = 112
COLS = 448
CUT = 896
A, B = 0, 1
SPAN = (pl.ds(0, CUT), pl.ds(CUT, WIDTH - CUT))
TILE = 896
NT = (((1,), (1,)), ((), ()))


def kernel(
    grad_ref, gate_ref, out_ref, rows, rows_o, cols, cols_o, stage,
    row_recv, rowo_recv, stage_recv, spread_recv, piece_recv, colo_recv, ssem,
):
    dp, tn = lax.axis_index("dp"), lax.axis_index("tensor")
    core, z, xh = lax.rem(dp, 2), lax.rem(lax.div(dp, 2), 8), lax.div(dp, 16)
    y, xl = lax.div(tn, 2), lax.rem(tn, 2)

    def device(h, k, c, t):
        return (h * 16 + k * 2 + c, t)

    def ring(value, size):
        return lax.rem(value + size, size)

    z_up = device(xh, ring(z + 1, 8), core, tn)
    z_dn = device(xh, ring(z - 1, 8), core, tn)
    x_far = device(1 - xh, z, core, tn)
    x_near = device(xh, z, core, y * 2 + 1 - xl)
    y_up = device(xh, z, core, ring(y + 1, 4) * 2 + xl)
    y_dn = device(xh, z, core, ring(y - 1, 4) * 2 + xl)
    other = device(xh, z, 1 - core, tn)

    def unit(h, k):
        return h * 8 + ring(k, 8)

    me = unit(xh, z)
    barrier = pltpu.get_barrier_semaphore()

    def greet(target):
        pl.semaphore_signal(barrier, inc=1, device_id=target, device_id_type=pl.DeviceIdType.MESH)

    def chip(t):
        return device(lax.div(t, 8), lax.rem(t, 8), core, tn)

    greet(other)
    for step in range(1, 8):
        greet(device(xh, z, core, ring(tn + step, 8)))
    for step in range(1, UNITS):
        greet(chip(ring(me + step, UNITS)))

    up_grad = (
        grad_ref[...].astype(jnp.float32) * jax.nn.silu(gate_ref[...].astype(jnp.float32))
    ).astype(jnp.bfloat16)
    rows[me] = up_grad.T

    pl.semaphore_wait(barrier, 23)

    sent = []

    def copy(src, dst, recv, target):
        made = pltpu.make_async_remote_copy(
            src_ref=src, dst_ref=dst, send_sem=ssem.at[len(sent)], recv_sem=recv,
            device_id=target, device_id_type=pl.DeviceIdType.MESH,
        )
        sent.append(None)
        return made

    waits = []

    def send(src, dst, recv, target):
        made = copy(src, dst, recv, target)
        made.start()
        waits.append(made.wait_send)

    def send_when(cond, src, dst, recv, target):
        made = copy(src, dst, recv, target)
        pl.when(cond)(made.start)
        waits.append(lambda: pl.when(cond)(made.wait_send))

    def arrive(ref, recv):
        pltpu.make_async_remote_copy(
            src_ref=ref, dst_ref=ref, send_sem=ssem.at[0], recv_sem=recv,
            device_id=other, device_id_type=pl.DeviceIdType.MESH,
        ).wait_recv()

    def row(kind, u, *targets):
        ref = rows.at[u, SPAN[kind]]
        for target in targets:
            send(ref, ref, row_recv.at[kind, u], target)
        send(ref, rows_o.at[u, SPAN[kind]], rowo_recv.at[kind, u], other)

    def row_in(kind, u, *targets):
        arrive(rows.at[u, SPAN[kind]], row_recv.at[kind, u])
        row(kind, u, *targets)

    def half(h):
        return pl.ds(h * 8, 8)

    def piece(e, h, *targets):
        src = cols.at[e, half(h)]
        for target in targets:
            send(src, src, piece_recv.at[e, h], target)
        slot = lax.rem(e, 4)
        send_when(
            lax.div(e, 4) != core, src, cols_o.at[slot, half(h)], colo_recv.at[slot, h], other
        )

    def piece_in(e, h, *targets):
        arrive(cols.at[e, half(h)], piece_recv.at[e, h])
        piece(e, h, *targets)

    def part(m, e):
        return pl.ds(pl.multiple_of(m * 896 + e * PIECE, PIECE), PIECE)

    for step in range(1, 8):
        e = ring(tn + step, 8)
        for m in range(2):
            send(
                rows.at[me, part(m, e)], stage.at[tn * 2 + m], stage_recv.at[tn * 2 + m],
                device(xh, z, core, e),
            )
    row(B, me, x_far, z_up, z_dn)
    for m in range(2):
        stage[tn * 2 + m] = rows[me, part(m, tn), :]

    def near(j):
        return unit(xh, z - j), unit(xh, z + j)

    def across(j):
        return unit(1 - xh, z - j), unit(1 - xh, z + j)

    def rows_b(pair, last=False):
        row_in(B, pair[0], *(() if last else (z_up,)))
        row_in(B, pair[1], z_dn)

    def rows_a(pair, last=False):
        row_in(A, pair[0], x_far, z_up)
        row_in(A, pair[1], x_far, *(() if last else (z_dn,)))

    def rows_far(pair, last=False):
        row_in(B, pair[0], z_up)
        row_in(B, pair[1], *(() if last else (z_dn,)))

    def rows_end(pair):
        row_in(A, pair[0])
        row_in(A, pair[1])

    for step in range(1, 8):
        e = ring(tn + step, 8)
        for m in range(2):
            arrive(stage.at[e * 2 + m], stage_recv.at[e * 2 + m])
    for step in range(1, 8):
        t = unit(xh, z + step)
        send(stage.at[t], cols.at[tn, me], spread_recv.at[me], chip(t))
    for step in range(8):
        t = unit(1 - xh, z + step)
        send(stage.at[t], cols.at[tn, me], spread_recv.at[me], chip(t))
    row(A, me, x_far, z_up, z_dn)
    cols[tn, me] = stage[me]

    far = unit(1 - xh, z)
    near_piece = y * 2 + 1 - xl
    dn, up, opp = ring(y - 1, 4) * 2, ring(y + 1, 4) * 2, ring(y + 2, 4) * 2

    def spread(h, first):
        for step in range(first, 8):
            u = unit(h, z + step)
            arrive(cols.at[tn, u], spread_recv.at[u])
        piece(tn, h, x_near, y_up, y_dn)

    def hop(h):
        piece_in(dn + xl, h, y_up)
        piece_in(up + xl, h)
        piece_in(dn + 1 - xl, h)
        piece_in(up + 1 - xl, h, y_dn)

    def end(h):
        piece_in(opp + xl, h)
        piece_in(opp + 1 - xl, h)

    rows_b(near(1))
    row_in(B, far, z_up, z_dn)
    spread(xh, 1)
    spread(1 - xh, 0)
    rows_a(near(1))
    rows_b(near(2))
    piece_in(near_piece, xh, y_up, y_dn)
    rows_far(across(1))
    piece_in(near_piece, 1 - xh, y_up, y_dn)
    rows_a(near(2))
    row_in(A, far)
    hop(xh)
    rows_b(near(3), last=True)
    rows_end(across(1))
    hop(1 - xh)
    rows_far(across(2))
    rows_end(across(2))

    last, far_last = unit(xh, z + 4), unit(1 - xh, z + 4)
    def ready(units):
        for u in units:
            for kind in (A, B):
                arrive(rows_o.at[u, SPAN[kind]], rowo_recv.at[kind, u])

    def multiply(units, first=False, last=False):
        ready(units)
        left = jnp.concatenate(
            [
                panel.reshape(COLS, TOK)
                for u in units
                for panel in (cols[pl.ds(core * 4, 4), u], cols_o[:, u])
            ],
            axis=1,
        )

        def tile(i, _):
            span = pl.ds(pl.multiple_of(i * TILE, TILE), TILE)
            right = jnp.concatenate([r[u, span, :] for u in units for r in (rows, rows_o)], axis=1)
            total = lax.dot_general(left, right, NT, preferred_element_type=jnp.float32)
            if not first:
                total = total + out_ref[:, span]
            if last:
                total = total * (1.0 / 4096)
            out_ref[:, span] = total
            return 0

        lax.fori_loop(0, WIDTH // TILE, tile, 0)

    def around(j):
        return [unit(h, k) for h in (xh, 1 - xh) for k in (z - j, z + j)]

    end(xh)
    end(1 - xh)
    for slot in range(4):
        for h in (xh, 1 - xh):
            arrive(cols_o.at[slot, half(h)], colo_recv.at[slot, h])
    multiply([me, far], first=True)
    rows_a(near(3), last=True)
    multiply(around(1))
    rows_far(across(3), last=True)
    multiply(around(2))
    row_in(B, last)
    row_in(A, last, x_far)
    rows_end(across(3))
    row_in(B, far_last)
    multiply(around(3))
    row_in(A, far_last)
    multiply([last, far_last], last=True)

    for wait in waits:
        wait()


def shards(grad_hidden, gate):
    vmem = pl.BlockSpec(memory_space=pltpu.VMEM)
    return pl.pallas_call(
        kernel,
        out_shape=jax.ShapeDtypeStruct((COLS, WIDTH), jnp.float32),
        in_specs=[vmem] * 2,
        out_specs=vmem,
        scratch_shapes=[
            pltpu.VMEM((UNITS, WIDTH, TOK), jnp.bfloat16),
            pltpu.VMEM((UNITS, WIDTH, TOK), jnp.bfloat16),
            pltpu.VMEM((8, UNITS, PIECE, TOK), jnp.bfloat16),
            pltpu.VMEM((4, UNITS, PIECE, TOK), jnp.bfloat16),
            pltpu.VMEM((UNITS, PIECE, TOK), jnp.bfloat16),
            pltpu.SemaphoreType.DMA((2, UNITS)),
            pltpu.SemaphoreType.DMA((2, UNITS)),
            pltpu.SemaphoreType.DMA((UNITS,)),
            pltpu.SemaphoreType.DMA((UNITS,)),
            pltpu.SemaphoreType.DMA((8, 2)),
            pltpu.SemaphoreType.DMA((4, 2)),
            pltpu.SemaphoreType.DMA((160,)),
        ],
        compiler_params=pltpu.CompilerParams(
            collective_id=0, has_side_effects=True, vmem_limit_bytes=30 * 1024 * 1024
        ),
    )(grad_hidden, gate).T


def solution(mesh):
    return jax.shard_map(
        shards,
        mesh=mesh,
        in_specs=(P("dp", "tensor"), P("dp", "tensor")),
        out_specs=P("tensor", "dp"),
        check_vma=False,
    )
```

time: 121 us -> 91.9 us (0.76)
  the two profiles are of different devices: /device:TPU:9 before, /device:TPU:1 now
where the time goes in v2:
time: 91.9 us; the launch traced here: 91.3 us
  Pallas kernels  87.5 us (95%)
  local copies, waits for them, and re-layouts  3.72 us (4%)
    pallas_call x1, Pallas kernels, shards(): pl.pallas_call(kernel, out_shape=jax.ShapeDtypeStruct((COLS, WIDTH), jnp....  87.5 us
    unnamed x5, local copies, waits for them, and re-layouts  3.72 us

profile of v2, /device:TPU:1, one launch (start us, length us, event | category | flops | bytes accessed | tf_op | source)
XLA Modules:
  0.0 91.3 jit_solution(2076765827531567837)
XLA Ops:
  0.0 0.0 copy-start
  0.0 1.0 %copy-done = bf16[128,1792]{1,0:T(8,128)(2,1)S(1)} copy-done((bf16[128,1792]{1,0:T(8,128)(2,1)S(1)}, bf16[128,1792]{1,0:T(8,128)(2,1)}, u32[]{:S(2)}) %copy-start) | copy-done | bytes 458776
  1.0 0.0 copy-start.1
  1.0 1.0 %copy-done.1 = bf16[128,1792]{1,0:T(8,128)(2,1)S(1)} copy-done((bf16[128,1792]{1,0:T(8,128)(2,1)S(1)}, bf16[128,1792]{1,0:T(8,128)(2,1)}, u32[]{:S(2)}) %copy-start.1) | copy-done | bytes 458776
  2.0 87.5 %shard_map.28 = f32[448,1792]{1,0:T(8,128)S(1)} custom-call(bf16[128,1792]{1,0:T(8,128)(2,1)S(1)} %copy-done, bf16[128,1792]{1,0:T(8,128)(2,1)S(1)} %copy-done.1), custom_call_target="tpu_custom_call" | custom-call | tf_op jit(solution)/shard_map/pallas_call | solution.py:265
  89.6 1.7 %copy.4 = f32[1792,448]{0,1:T(8,128)} copy(f32[1792,448]{0,1:T(8,128)S(1)} %bitcast.1) | data formatting | bytes 6422528
Async XLA Ops:
  0.0 1.0 %copy-start = (bf16[128,1792]{1,0:T(8,128)(2,1)S(1)}, bf16[128,1792]{1,0:T(8,128)(2,1)}, u32[]{:S(2)}) copy-start(bf16[128,1792]{1,0:T(8,128)(2,1)} %grad_ref.1) | copy-start | bytes 1376260
  1.0 1.0 %copy-start.1 = (bf16[128,1792]{1,0:T(8,128)(2,1)S(1)}, bf16[128,1792]{1,0:T(8,128)(2,1)}, u32[]{:S(2)}) copy-start(bf16[128,1792]{1,0:T(8,128)(2,1)} %gate_ref.1) | copy-start | bytes 1376260

commit v3 on v0

v3 whole, which is shorter than its diff:
```python
import jax
import jax.numpy as jnp
from jax import lax
from jax.experimental import pallas as pl
from jax.experimental.pallas import tpu as pltpu
from jax.sharding import PartitionSpec as P

WIDTH = 1792
TOK = 128
UNITS = 16
PIECE = 112
COLS = 448
A, B, C, D = range(4)
SPAN = (pl.ds(0, 896), pl.ds(896, 896), pl.ds(896, 448), pl.ds(1344, 448))
NT = (((1,), (1,)), ((), ()))


def kernel(
    grad_hbm, gate_hbm, out_ref, grad_ref, gate_ref, rows, rows_o, cols, cols_o, stage,
    row_recv, split_recv, rowo_recv, stage_recv, spread_recv, piece_recv, colo_recv, sent, load_sem,
):
    dp, tn = lax.axis_index("dp"), lax.axis_index("tensor")
    core, z, xh = lax.rem(dp, 2), lax.rem(lax.div(dp, 2), 8), lax.div(dp, 16)
    y, xl = lax.div(tn, 2), lax.rem(tn, 2)

    def device(h, k, c, t):
        return (h * 16 + k * 2 + c, t)

    def ring(value, size):
        return lax.rem(value + size, size)

    z_up = device(xh, ring(z + 1, 8), core, tn)
    z_dn = device(xh, ring(z - 1, 8), core, tn)
    x_far = device(1 - xh, z, core, tn)
    x_near = device(xh, z, core, y * 2 + 1 - xl)
    y_up = device(xh, z, core, ring(y + 1, 4) * 2 + xl)
    y_dn = device(xh, z, core, ring(y - 1, 4) * 2 + xl)
    other = device(xh, z, 1 - core, tn)

    def unit(h, k):
        return h * 8 + ring(k, 8)

    me = unit(xh, z)
    loads = [
        pltpu.make_async_copy(src, dst, load_sem.at[i])
        for i, (src, dst) in enumerate(((grad_hbm, grad_ref), (gate_hbm, gate_ref)))
    ]
    for load in loads:
        load.start()

    barrier = pltpu.get_barrier_semaphore()

    def greet(target):
        pl.semaphore_signal(barrier, inc=1, device_id=target, device_id_type=pl.DeviceIdType.MESH)

    def chip(t):
        return device(lax.div(t, 8), lax.rem(t, 8), core, tn)

    greet(other)
    for step in range(1, 8):
        greet(device(xh, z, core, ring(tn + step, 8)))
    for step in range(1, UNITS):
        greet(chip(ring(me + step, UNITS)))

    for load in loads:
        load.wait()
    up_grad = (
        grad_ref[...].astype(jnp.float32) * jax.nn.silu(gate_ref[...].astype(jnp.float32))
    ).astype(jnp.bfloat16)
    rows[me] = up_grad.T

    pl.semaphore_wait(barrier, 23)

    ROW, ROW_O, SCATTER, SPREAD, PLANE, PLANE_O = (sent.at[i] for i in range(6))

    def copy(src, dst, send, recv, target):
        return pltpu.make_async_remote_copy(
            src_ref=src, dst_ref=dst, send_sem=send, recv_sem=recv,
            device_id=target, device_id_type=pl.DeviceIdType.MESH,
        )

    def arrive(ref, recv):
        copy(ref, ref, sent.at[0], recv, other).wait_recv()

    def leave(ref, send):
        copy(ref, ref, send, load_sem.at[0], other).wait_send()

    def pass_on(kind, u, *targets, recv=None):
        ref = rows.at[u, SPAN[kind]]
        for target in targets:
            copy(ref, ref, ROW, row_recv.at[kind, u] if recv is None else recv, target).start()

    def share(kind, u, group):
        copy(
            rows.at[u, SPAN[kind]], rows_o.at[u, SPAN[kind]], ROW_O,
            rowo_recv.at[min(kind, B), group], other,
        ).start()

    def row_in(kind, u, group, *targets):
        arrive(rows.at[u, SPAN[kind]], row_recv.at[kind, u])
        pass_on(kind, u, *targets)
        share(kind, u, group)

    def half(h):
        return pl.ds(h * 8, 8)

    def piece(e, h, *targets):
        src = cols.at[e, half(h)]
        for target in targets:
            copy(src, src, PLANE, piece_recv.at[e, h], target).start()

        @pl.when(lax.div(e, 4) != core)
        def _():
            copy(src, cols_o.at[lax.rem(e, 4), half(h)], PLANE_O, colo_recv, other).start()

    def piece_in(e, h, *targets):
        arrive(cols.at[e, half(h)], piece_recv.at[e, h])
        piece(e, h, *targets)

    def part(m, e):
        return pl.ds(pl.multiple_of(m * 896 + e * PIECE, PIECE), PIECE)

    for step in range(1, 8):
        e = ring(tn + step, 8)
        for m in range(2):
            copy(
                rows.at[me, part(m, e)], stage.at[tn * 2 + m], SCATTER, stage_recv,
                device(xh, z, core, e),
            ).start()
    pass_on(A, me, z_up, z_dn)
    pass_on(B, me, x_far)
    pass_on(C, me, z_up, recv=split_recv.at[0, 0])
    pass_on(C, me, z_dn, recv=split_recv.at[0, 1])
    pass_on(A, me, x_far)
    share(A, me, 0)
    share(B, me, 0)
    for m in range(2):
        stage[tn * 2 + m] = rows[me, part(m, tn), :]

    arrive(stage.at[pl.ds(0, 14)], stage_recv)
    for h, first in ((xh, 1), (1 - xh, 0)):
        for step in range(first, 8):
            t = unit(h, z + step)
            copy(stage.at[t], cols.at[tn, me], SPREAD, spread_recv.at[first], chip(t)).start()
    pass_on(D, me, z_up, recv=split_recv.at[1, 0])
    pass_on(D, me, z_dn, recv=split_recv.at[1, 1])
    cols[tn, me] = stage[me]

    far, last, far_last = unit(1 - xh, z), unit(xh, z + 4), unit(1 - xh, z + 4)
    near_piece = y * 2 + 1 - xl
    dn, up, opp = ring(y - 1, 4) * 2, ring(y + 1, 4) * 2, ring(y + 2, 4) * 2

    def lo(j):
        return unit(xh, z - j)

    def hi(j):
        return unit(xh, z + j)

    def far_lo(j):
        return unit(1 - xh, z - j)

    def far_hi(j):
        return unit(1 - xh, z + j)

    def spread(h, first):
        arrive(stage.at[pl.ds(0, 8 - first)], spread_recv.at[first])
        piece(tn, h, x_near, y_up, y_dn)

    def hop(h):
        piece_in(dn + xl, h, y_up)
        piece_in(up + xl, h)
        piece_in(dn + 1 - xl, h)
        piece_in(up + 1 - xl, h, y_dn)

    def end(h):
        piece_in(opp + xl, h)
        piece_in(opp + 1 - xl, h)

    def split_in(u, side, target):
        arrive(rows.at[u, SPAN[C]], split_recv.at[0, side])
        arrive(rows.at[u, SPAN[D]], split_recv.at[1, side])
        pass_on(B, u, target)
        share(B, u, 0)

    groups = [[me, far]] + [[lo(j), hi(j), far_lo(j), far_hi(j)] for j in range(1, 4)]
    groups = [groups[0] + groups[1], groups[2], groups[3], [last, far_last]]

    def multiply(kind, g):
        units = groups[g]
        arrive(rows_o.at[pl.ds(0, len(units) // 2)], rowo_recv.at[kind, g])
        left = jnp.concatenate(
            [
                panel.reshape(COLS, TOK)
                for u in units
                for panel in (cols[pl.ds(core * 4, 4), u], cols_o[:, u])
            ],
            axis=1,
        )
        right = jnp.concatenate([r[u, SPAN[kind], :] for u in units for r in (rows, rows_o)], axis=1)
        total = lax.dot_general(left, right, NT, preferred_element_type=jnp.float32)
        if g > 0:
            total = total + out_ref[:, SPAN[kind]]
        if g == 3:
            total = total * (1.0 / 4096)
        out_ref[:, SPAN[kind]] = total

    row_in(A, lo(1), 0, z_up)
    row_in(A, hi(1), 0, z_dn)
    row_in(B, far, 0, z_up, z_dn)
    spread(xh, 1)
    spread(1 - xh, 0)
    pass_on(A, lo(1), x_far)
    pass_on(A, hi(1), x_far)
    row_in(A, far, 0)
    piece_in(near_piece, xh, y_up, y_dn)
    row_in(A, lo(2), 1, z_up, x_far)
    row_in(A, hi(2), 1, z_dn, x_far)
    piece_in(near_piece, 1 - xh, y_up, y_dn)
    split_in(hi(1), 1, z_dn)
    row_in(B, far_lo(1), 0, z_up)
    row_in(B, far_hi(1), 0, z_dn)
    hop(xh)
    row_in(A, lo(3), 2, z_up, x_far)
    row_in(A, hi(3), 2, x_far)
    split_in(lo(1), 0, z_up)
    hop(1 - xh)
    row_in(A, far_lo(1), 0)
    row_in(A, far_hi(1), 0)
    row_in(B, hi(2), 1, z_dn)
    row_in(B, far_lo(2), 1, z_up)
    end(xh)
    row_in(B, far_hi(2), 1, z_dn)
    row_in(A, last, 3, x_far)
    end(1 - xh)
    arrive(cols_o, colo_recv)
    multiply(A, 0)
    row_in(B, lo(2), 1, z_up)
    row_in(A, far_lo(2), 1)
    row_in(A, far_hi(2), 1)
    multiply(B, 0)
    row_in(B, hi(3), 2, z_dn)
    multiply(A, 1)
    row_in(B, far_lo(3), 2)
    pass_on(C, far_lo(3), z_up, recv=split_recv.at[0, 2])
    row_in(B, far_hi(3), 2)
    pass_on(D, far_hi(3), z_dn, recv=split_recv.at[1, 2])
    multiply(B, 1)
    row_in(A, far_lo(3), 2)
    row_in(A, far_hi(3), 2)
    multiply(A, 2)
    row_in(B, lo(3), 2)
    row_in(B, last, 3)
    row_in(A, far_last, 3)
    for kind in (C, D):
        arrive(rows.at[far_last, SPAN[kind]], split_recv.at[kind - C, 2])
        share(kind, far_last, 3)
    multiply(B, 2)
    multiply(A, 3)
    multiply(B, 3)

    leave(rows.at[pl.ds(0, 15)], ROW)
    leave(rows, ROW_O)
    leave(stage.at[pl.ds(0, 14)], SCATTER)
    leave(stage.at[pl.ds(0, 15)], SPREAD)
    leave(cols.at[pl.ds(0, 7)], PLANE)
    leave(cols_o, PLANE_O)


def shards(grad_hidden, gate):
    dma = pltpu.SemaphoreType.DMA
    return pl.pallas_call(
        kernel,
        out_shape=jax.ShapeDtypeStruct((COLS, WIDTH), jnp.float32),
        in_specs=[pl.BlockSpec(memory_space=pltpu.HBM)] * 2,
        out_specs=pl.BlockSpec(memory_space=pltpu.VMEM),
        scratch_shapes=[
            pltpu.VMEM((TOK, WIDTH), jnp.bfloat16),
            pltpu.VMEM((TOK, WIDTH), jnp.bfloat16),
            pltpu.VMEM((UNITS, WIDTH, TOK), jnp.bfloat16),
            pltpu.VMEM((UNITS, WIDTH, TOK), jnp.bfloat16),
            pltpu.VMEM((8, UNITS, PIECE, TOK), jnp.bfloat16),
            pltpu.VMEM((4, UNITS, PIECE, TOK), jnp.bfloat16),
            pltpu.VMEM((UNITS, PIECE, TOK), jnp.bfloat16),
            dma((2, UNITS)),
            dma((2, 3)),
            dma((2, 4)),
            dma,
            dma((2,)),
            dma((8, 2)),
            dma,
            dma((6,)),
            dma((2,)),
        ],
        compiler_params=pltpu.CompilerParams(
            collective_id=0, has_side_effects=True, vmem_limit_bytes=40_000_000
        ),
    )(*(pltpu.with_memory_space_constraint(a, pltpu.HBM) for a in (grad_hidden, gate))).T


def solution(mesh):
    return jax.shard_map(
        shards,
        mesh=mesh,
        in_specs=(P("dp", "tensor"), P("dp", "tensor")),
        out_specs=P("tensor", "dp"),
        check_vma=False,
    )
```

time: 353 us -> 81 us (0.23)
  waiting for transfers between devices: 316 us -> 0 us
  Pallas kernels: 0 us -> 79.2 us
  matrix products: 13.4 us -> 0 us
  between operations: 13.4 us -> 0.01 us
  other arithmetic: 9.53 us -> 0 us
    psum x1 -> x0, waiting for transfers between devices: 184 us -> none  [broadcast(): return lax.psum(block, axis)]
    all_gather x1 -> x0, waiting for transfers between devices: 132 us -> none  [shards(): rows_all = lax.all_gather(up_grad, 'dp', axis=0, tiled=True)]
    pallas_call x0 -> x1, Pallas kernels: none -> 79.2 us  [shards(): pl.pallas_call(kernel, out_shape=jax.ShapeDtypeStruct((COLS, WIDTH), jnp....]
    dot_general x1 -> x0, matrix products: 13.4 us -> none  [shards(): lax.dot_general(rows_all, cols_all, contract, preferred_element_type=jnp....]
    select_n x1 -> x0, other arithmetic: 7.33 us -> none  [broadcast(): jnp.where(lax.axis_index(axis) == owner, block, jnp.zeros_like(block))]
  transfers between devices with their start and end apart: 2 -> 0, of which waited for: 2 -> 0; matrix products, arithmetic and copies ran while one was open for 0% -> 0% of each run, Pallas kernels for 0% -> 0%
where the time goes in v3:
time: 81 us; the launch traced here: 80.9 us
  Pallas kernels  79.2 us (98%)
  local copies, waits for them, and re-layouts  1.69 us (2%)
    pallas_call x1, Pallas kernels, shards(): pl.pallas_call(kernel, out_shape=jax.ShapeDtypeStruct((COLS, WIDTH), jnp....  79.2 us
    unnamed x1, local copies, waits for them, and re-layouts  1.69 us

profile of v3, /device:TPU:1, one launch (start us, length us, event | category | flops | bytes accessed | tf_op | source)
XLA Modules:
  0.0 80.9 jit_solution(9916189117181347367)
XLA Ops:
  0.0 79.2 %shard_map.28 = f32[448,1792]{1,0:T(8,128)S(1)} custom-call(bf16[128,1792]{1,0:T(8,128)(2,1)} %grad_hbm.1, bf16[128,1792]{1,0:T(8,128)(2,1)} %gate_hbm.1), custom_call_target="tpu_custom_call" | custom-call | tf_op jit(solution)/shard_map/pallas_call | solution.py:271
  79.2 1.7 %copy.4 = f32[1792,448]{0,1:T(8,128)} copy(f32[1792,448]{0,1:T(8,128)S(1)} %bitcast.1) | data formatting | bytes 6422528

commit v4 on v3

--- a/solution.py
+++ b/solution.py
@@ -11,7 +11,9 @@
 PIECE = 112
 COLS = 448
 A, B, C, D = range(4)
-SPAN = (pl.ds(0, 896), pl.ds(896, 896), pl.ds(896, 448), pl.ds(1344, 448))
+CUT, HALF = 864, 464
+SPAN = (pl.ds(0, CUT), pl.ds(CUT, 2 * HALF), pl.ds(CUT, HALF), pl.ds(CUT + HALF, HALF))
+PART = (pl.ds(0, 768), pl.ds(768, WIDTH - 768))
 NT = (((1,), (1,)), ((), ()))
 
 
@@ -187,7 +189,7 @@
 
     def multiply(kind, g):
         units = groups[g]
-        arrive(rows_o.at[pl.ds(0, len(units) // 2)], rowo_recv.at[kind, g])
+        arrive(rows_o.at[pl.ds(0, len(units)), SPAN[kind]], rowo_recv.at[kind, g])
         left = jnp.concatenate(
             [
                 panel.reshape(COLS, TOK)
@@ -196,13 +198,13 @@
             ],
             axis=1,
         )
-        right = jnp.concatenate([r[u, SPAN[kind], :] for u in units for r in (rows, rows_o)], axis=1)
+        right = jnp.concatenate([r[u, PART[kind], :] for u in units for r in (rows, rows_o)], axis=1)
         total = lax.dot_general(left, right, NT, preferred_element_type=jnp.float32)
         if g > 0:
-            total = total + out_ref[:, SPAN[kind]]
+            total = total + out_ref[:, PART[kind]]
         if g == 3:
             total = total * (1.0 / 4096)
-        out_ref[:, SPAN[kind]] = total
+        out_ref[:, PART[kind]] = total
 
     row_in(A, lo(1), 0, z_up)
     row_in(A, hi(1), 0, z_dn)
@@ -211,45 +213,45 @@
     spread(1 - xh, 0)
     pass_on(A, lo(1), x_far)
     pass_on(A, hi(1), x_far)
-    row_in(A, far, 0)
-    piece_in(near_piece, xh, y_up, y_dn)
     row_in(A, lo(2), 1, z_up, x_far)
     row_in(A, hi(2), 1, z_dn, x_far)
-    piece_in(near_piece, 1 - xh, y_up, y_dn)
+    piece_in(near_piece, xh, y_up, y_dn)
+    row_in(A, far, 0)
     split_in(hi(1), 1, z_dn)
     row_in(B, far_lo(1), 0, z_up)
     row_in(B, far_hi(1), 0, z_dn)
-    hop(xh)
+    piece_in(near_piece, 1 - xh, y_up, y_dn)
     row_in(A, lo(3), 2, z_up, x_far)
     row_in(A, hi(3), 2, x_far)
     split_in(lo(1), 0, z_up)
-    hop(1 - xh)
+    hop(xh)
+    row_in(B, hi(2), 1, z_dn)
     row_in(A, far_lo(1), 0)
     row_in(A, far_hi(1), 0)
-    row_in(B, hi(2), 1, z_dn)
     row_in(B, far_lo(2), 1, z_up)
-    end(xh)
+    hop(1 - xh)
     row_in(B, far_hi(2), 1, z_dn)
     row_in(A, last, 3, x_far)
+    end(xh)
+    row_in(B, lo(2), 1, z_up)
     end(1 - xh)
+    row_in(B, hi(3), 2, z_dn)
     arrive(cols_o, colo_recv)
     multiply(A, 0)
-    row_in(B, lo(2), 1, z_up)
     row_in(A, far_lo(2), 1)
     row_in(A, far_hi(2), 1)
     multiply(B, 0)
-    row_in(B, hi(3), 2, z_dn)
-    multiply(A, 1)
     row_in(B, far_lo(3), 2)
     pass_on(C, far_lo(3), z_up, recv=split_recv.at[0, 2])
     row_in(B, far_hi(3), 2)
     pass_on(D, far_hi(3), z_dn, recv=split_recv.at[1, 2])
+    multiply(A, 1)
     multiply(B, 1)
     row_in(A, far_lo(3), 2)
     row_in(A, far_hi(3), 2)
-    multiply(A, 2)
     row_in(B, lo(3), 2)
     row_in(B, last, 3)
+    multiply(A, 2)
     row_in(A, far_last, 3)
     for kind in (C, D):
         arrive(rows.at[far_last, SPAN[kind]], split_recv.at[kind - C, 2])

time: 81 us -> 80.5 us (level)
  no operation moved by 1% of the time
where the time goes in v4:
time: 80.5 us; the launch traced here: 80.4 us
  Pallas kernels  78.7 us (98%)
  local copies, waits for them, and re-layouts  1.69 us (2%)
    pallas_call x1, Pallas kernels, shards(): pl.pallas_call(kernel, out_shape=jax.ShapeDtypeStruct((COLS, WIDTH), jnp....  78.7 us
    unnamed x1, local copies, waits for them, and re-layouts  1.69 us

profile of v4, /device:TPU:1, one launch (start us, length us, event | category | flops | bytes accessed | tf_op | source)
XLA Modules:
  0.0 80.4 jit_solution(16381262505272790374)
XLA Ops:
  0.0 78.7 %shard_map.28 = f32[448,1792]{1,0:T(8,128)S(1)} custom-call(bf16[128,1792]{1,0:T(8,128)(2,1)} %grad_hbm.1, bf16[128,1792]{1,0:T(8,128)(2,1)} %gate_hbm.1), custom_call_target="tpu_custom_call" | custom-call | tf_op jit(solution)/shard_map/pallas_call | solution.py:273
  78.7 1.7 %copy.4 = f32[1792,448]{0,1:T(8,128)} copy(f32[1792,448]{0,1:T(8,128)S(1)} %bitcast.1) | data formatting | bytes 6422528

commit v5 on v4

--- a/solution.py
+++ b/solution.py
@@ -131,8 +131,7 @@
             ).start()
     pass_on(A, me, z_up, z_dn)
     pass_on(B, me, x_far)
-    pass_on(C, me, z_up, recv=split_recv.at[0, 0])
-    pass_on(C, me, z_dn, recv=split_recv.at[0, 1])
+    pass_on(B, me, z_up, z_dn)
     pass_on(A, me, x_far)
     share(A, me, 0)
     share(B, me, 0)
@@ -144,8 +143,6 @@
         for step in range(first, 8):
             t = unit(h, z + step)
             copy(stage.at[t], cols.at[tn, me], SPREAD, spread_recv.at[first], chip(t)).start()
-    pass_on(D, me, z_up, recv=split_recv.at[1, 0])
-    pass_on(D, me, z_dn, recv=split_recv.at[1, 1])
     cols[tn, me] = stage[me]
 
     far, last, far_last = unit(1 - xh, z), unit(xh, z + 4), unit(1 - xh, z + 4)
@@ -177,12 +174,6 @@
     def end(h):
         piece_in(opp + xl, h)
         piece_in(opp + 1 - xl, h)
-
-    def split_in(u, side, target):
-        arrive(rows.at[u, SPAN[C]], split_recv.at[0, side])
-        arrive(rows.at[u, SPAN[D]], split_recv.at[1, side])
-        pass_on(B, u, target)
-        share(B, u, 0)
 
     groups = [[me, far]] + [[lo(j), hi(j), far_lo(j), far_hi(j)] for j in range(1, 4)]
     groups = [groups[0] + groups[1], groups[2], groups[3], [last, far_last]]
@@ -217,13 +208,13 @@
     row_in(A, hi(2), 1, z_dn, x_far)
     piece_in(near_piece, xh, y_up, y_dn)
     row_in(A, far, 0)
-    split_in(hi(1), 1, z_dn)
+    row_in(B, hi(1), 0, z_dn)
     row_in(B, far_lo(1), 0, z_up)
     row_in(B, far_hi(1), 0, z_dn)
     piece_in(near_piece, 1 - xh, y_up, y_dn)
     row_in(A, lo(3), 2, z_up, x_far)
     row_in(A, hi(3), 2, x_far)
-    split_in(lo(1), 0, z_up)
+    row_in(B, lo(1), 0, z_up)
     hop(xh)
     row_in(B, hi(2), 1, z_dn)
     row_in(A, far_lo(1), 0)
@@ -242,9 +233,9 @@
     row_in(A, far_hi(2), 1)
     multiply(B, 0)
     row_in(B, far_lo(3), 2)
-    pass_on(C, far_lo(3), z_up, recv=split_recv.at[0, 2])
+    pass_on(C, far_lo(3), z_up, recv=split_recv.at[0])
     row_in(B, far_hi(3), 2)
-    pass_on(D, far_hi(3), z_dn, recv=split_recv.at[1, 2])
+    pass_on(D, far_hi(3), z_dn, recv=split_recv.at[1])
     multiply(A, 1)
     multiply(B, 1)
     row_in(A, far_lo(3), 2)
@@ -254,7 +245,7 @@
     multiply(A, 2)
     row_in(A, far_last, 3)
     for kind in (C, D):
-        arrive(rows.at[far_last, SPAN[kind]], split_recv.at[kind - C, 2])
+        arrive(rows.at[far_last, SPAN[kind]], split_recv.at[kind - C])
         share(kind, far_last, 3)
     multiply(B, 2)
     multiply(A, 3)
@@ -284,7 +275,7 @@
             pltpu.VMEM((4, UNITS, PIECE, TOK), jnp.bfloat16),
             pltpu.VMEM((UNITS, PIECE, TOK), jnp.bfloat16),
             dma((2, UNITS)),
-            dma((2, 3)),
+            dma((2,)),
             dma((2, 4)),
             dma,
             dma((2,)),

time: 80.5 us -> 79.7 us (0.990)
    pallas_call x1, Pallas kernels: 78.7 us -> 77.9 us  [shards(): pl.pallas_call(kernel, out_shape=jax.ShapeDtypeStruct((COLS, WIDTH), jnp....]
where the time goes in v5:
time: 79.7 us; the launch traced here: 79.6 us
  Pallas kernels  77.9 us (98%)
  local copies, waits for them, and re-layouts  1.69 us (2%)
    pallas_call x1, Pallas kernels, shards(): pl.pallas_call(kernel, out_shape=jax.ShapeDtypeStruct((COLS, WIDTH), jnp....  77.9 us
    unnamed x1, local copies, waits for them, and re-layouts  1.69 us

profile of v5, /device:TPU:1, one launch (start us, length us, event | category | flops | bytes accessed | tf_op | source)
XLA Modules:
  0.0 79.6 jit_solution(386989649528918693)
XLA Ops:
  0.0 77.9 %shard_map.28 = f32[448,1792]{1,0:T(8,128)S(1)} custom-call(bf16[128,1792]{1,0:T(8,128)(2,1)} %grad_hbm.1, bf16[128,1792]{1,0:T(8,128)(2,1)} %gate_hbm.1), custom_call_target="tpu_custom_call" | custom-call | tf_op jit(solution)/shard_map/pallas_call | solution.py:264
  77.9 1.7 %copy.4 = f32[1792,448]{0,1:T(8,128)} copy(f32[1792,448]{0,1:T(8,128)S(1)} %bitcast.1) | data formatting | bytes 6422528

commit v6 on v5

--- a/solution.py
+++ b/solution.py
@@ -204,9 +204,9 @@
     spread(1 - xh, 0)
     pass_on(A, lo(1), x_far)
     pass_on(A, hi(1), x_far)
+    piece_in(near_piece, xh, y_up, y_dn)
     row_in(A, lo(2), 1, z_up, x_far)
     row_in(A, hi(2), 1, z_dn, x_far)
-    piece_in(near_piece, xh, y_up, y_dn)
     row_in(A, far, 0)
     row_in(B, hi(1), 0, z_dn)
     row_in(B, far_lo(1), 0, z_up)

time: 79.7 us -> 79.7 us (level)
  no operation moved by 1% of the time
where the time goes in v6:
time: 79.7 us; the launch traced here: 79.6 us
  Pallas kernels  77.9 us (98%)
  local copies, waits for them, and re-layouts  1.69 us (2%)
    pallas_call x1, Pallas kernels, shards(): pl.pallas_call(kernel, out_shape=jax.ShapeDtypeStruct((COLS, WIDTH), jnp....  77.9 us
    unnamed x1, local copies, waits for them, and re-layouts  1.69 us

profile of v6, /device:TPU:1, one launch (start us, length us, event | category | flops | bytes accessed | tf_op | source)
XLA Modules:
  0.0 79.6 jit_solution(17541387161106244409)
XLA Ops:
  0.0 77.9 %shard_map.28 = f32[448,1792]{1,0:T(8,128)S(1)} custom-call(bf16[128,1792]{1,0:T(8,128)(2,1)} %grad_hbm.1, bf16[128,1792]{1,0:T(8,128)(2,1)} %gate_hbm.1), custom_call_target="tpu_custom_call" | custom-call | tf_op jit(solution)/shard_map/pallas_call | solution.py:264
  77.9 1.7 %copy.4 = f32[1792,448]{0,1:T(8,128)} copy(f32[1792,448]{0,1:T(8,128)S(1)} %bitcast.1) | data formatting | bytes 6422528

commit v7 on v6

--- a/solution.py
+++ b/solution.py
@@ -140,7 +140,7 @@
 
     arrive(stage.at[pl.ds(0, 14)], stage_recv)
     for h, first in ((xh, 1), (1 - xh, 0)):
-        for step in range(first, 8):
+        for step in (4, 3, 5, 2, 6, 1, 7, 0)[: 8 - first]:
             t = unit(h, z + step)
             copy(stage.at[t], cols.at[tn, me], SPREAD, spread_recv.at[first], chip(t)).start()
     cols[tn, me] = stage[me]

time: 79.7 us -> 79.7 us (level)
  no operation moved by 1% of the time
where the time goes in v7:
time: 79.7 us; the launch traced here: 79.6 us
  Pallas kernels  77.9 us (98%)
  local copies, waits for them, and re-layouts  1.69 us (2%)
    pallas_call x1, Pallas kernels, shards(): pl.pallas_call(kernel, out_shape=jax.ShapeDtypeStruct((COLS, WIDTH), jnp....  77.9 us
    unnamed x1, local copies, waits for them, and re-layouts  1.69 us

profile of v7, /device:TPU:1, one launch (start us, length us, event | category | flops | bytes accessed | tf_op | source)
XLA Modules:
  0.0 79.6 jit_solution(15897589174729716983)
XLA Ops:
  0.0 77.9 %shard_map.28 = f32[448,1792]{1,0:T(8,128)S(1)} custom-call(bf16[128,1792]{1,0:T(8,128)(2,1)} %grad_hbm.1, bf16[128,1792]{1,0:T(8,128)(2,1)} %gate_hbm.1), custom_call_target="tpu_custom_call" | custom-call | tf_op jit(solution)/shard_map/pallas_call | solution.py:264
  77.9 1.7 %copy.4 = f32[1792,448]{0,1:T(8,128)} copy(f32[1792,448]{0,1:T(8,128)S(1)} %bitcast.1) | data formatting | bytes 6422528
